TPU v7x, 256 devices: a whole 4x4x8 slice. The times are simulated.
256 devices in a mesh: batch: 8 (over z), seq: 32 (over y, x, core).
Axes of the slice: x: 4, y: 4, z: 8, core: 2. Of those that a mesh axis runs over, the one named last changes fastest.
Arguments:
- hidden: bfloat16 [8, 16384, 4096], P('batch', 'seq'), may hold values from -6 to 6
- score_direction: bfloat16 [8, 16384, 4096], P('batch', 'seq'), may hold values from -6 to 6
- adapter_down: bfloat16 [4096, 256], replicated, may hold values from -0.09375 to 0.09375
- adapter_up: bfloat16 [4096, 256], replicated, may hold values from -0.09375 to 0.09375
- rewards: float32 [8, 16384], P('batch', 'seq'), may hold values from -0.3125 to 0.3125
- values: float32 [8, 16384], P('batch', 'seq'), may hold values from -120 to 120
- log_ratio: float32 [8, 16384], P('batch', 'seq'), may hold values from -4 to 4
- lengths: int32 [8], P('batch'), may hold values from 4096 to 16384
Outputs:
- returns: float32 [8, 16384], P('batch', 'seq')
- grad_down: float32 [4096, 256], P(('batch', 'seq'))
- grad_up: float32 [4096, 256], P(('batch', 'seq'))
All inputs are finite; a program needn't handle non-finite values.
Results may differ from a plain program's by a relative error of at most 0.0029.
Values sent between devices are 32-bit elements; how exact they have to be, the bound alone decides.
A program may use at most 128 MiB of HBM per device.

v0:
```python
import math

import jax
import jax.numpy as jnp
from jax import lax
from jax.sharding import PartitionSpec as P

ratio_cap = 2.0
weight_gain = 0.08


def sent_to_all(shard, axis):
    devices = lax.axis_size(axis)
    return lax.all_to_all(
        jnp.broadcast_to(shard[None], (devices, *shard.shape)), axis, 0, 0, tiled=True
    )


def laid_out(blocks, dim):
    blocks = jnp.moveaxis(blocks, 0, dim)
    dims = blocks.shape
    return blocks.reshape(*dims[:dim], dims[dim] * dims[dim + 1], *dims[dim + 2 :])


def gather_directly(shard, axis, dim):
    blocks = sent_to_all(shard, axis)
    return laid_out(blocks, dim)


def local(hidden, score_direction, adapter_down, adapter_up, rewards, values, log_ratio, lengths):
    seq_count, shard_len, model_width = hidden.shape
    low_rank_product = adapter_down.shape[1]
    shard_total = lax.axis_size("seq")
    total_len = shard_len * shard_total
    seq_total = seq_count * lax.axis_size("batch")
    shard_id = lax.axis_index("seq")
    inner = jnp.arange(shard_len, dtype=jnp.int32)
    positions = shard_id * shard_len + inner
    valid = (positions[None, :] < lengths[:, None]).astype(jnp.float32)
    adapter_scale = 1.0 / math.sqrt(low_rank_product)
    down_projected = jnp.einsum(
        "ogz,zw->ogw", hidden, adapter_down, preferred_element_type=jnp.float32
    )
    up_projected = jnp.einsum(
        "ogz,zw->ogw", score_direction, adapter_up, preferred_element_type=jnp.float32
    )
    weight_update = adapter_scale * jnp.sum(down_projected * up_projected, axis=-1)
    importance = jnp.exp(log_ratio + weight_update)
    live = rewards * valid
    offsets = (inner[None, :] - inner[:, None]).astype(jnp.float32)
    discount_mat = jnp.where(offsets >= 0, jnp.exp(-offsets / total_len), jnp.zeros_like(offsets))
    within = jnp.einsum("sk,tk->st", live, discount_mat, precision=lax.Precision.HIGHEST)
    firsts = within[:, 0]
    every_first = gather_directly(firsts[:, None], "seq", 1)
    blocks = jnp.arange(shard_total, dtype=jnp.int32)
    steps_back = (blocks - shard_id - 1).astype(jnp.float32)
    weights_blk = jnp.where(
        blocks > shard_id, jnp.exp(-steps_back * shard_len / total_len), jnp.zeros_like(steps_back)
    )
    carried = jnp.sum(every_first * weights_blk[None, :], axis=1)
    tail_decay = jnp.exp(-(shard_len - inner).astype(jnp.float32) / total_len)
    returns = within + tail_decay[None, :] * carried[:, None]
    advantage = returns - values
    seq_weight = (
        weight_gain
        * math.sqrt(total_len * low_rank_product / seq_total)
        / lengths.astype(jnp.float32)
    )
    token_weights = valid * jnp.minimum(importance, ratio_cap) * advantage * seq_weight[:, None]
    up_scaled_map = (-adapter_scale * token_weights[:, :, None] * up_projected).astype(jnp.bfloat16)
    down_scaled_map = (-adapter_scale * token_weights[:, :, None] * down_projected).astype(
        jnp.bfloat16
    )
    group_total = lax.axis_size(("batch", "seq"))
    own_rows = model_width // group_total
    clip_norm = 0.5 * math.sqrt(2.0 * model_width * low_rank_product)
    partial_terms = jnp.concatenate(
        [
            jnp.einsum("oxe,oxq->eq", hidden, up_scaled_map, preferred_element_type=jnp.float32),
            jnp.einsum(
                "oxe,oxq->eq", score_direction, down_scaled_map, preferred_element_type=jnp.float32
            ),
        ],
        axis=1,
    )
    summed = lax.psum(partial_terms, ("batch", "seq"))
    squares = jnp.sum(summed * summed)
    own_part = lax.dynamic_slice_in_dim(
        summed, lax.axis_index(("batch", "seq")) * own_rows, own_rows, 0
    )
    grad_norm = jnp.sqrt(squares)
    factor = clip_norm / jnp.maximum(grad_norm, clip_norm)
    return (
        returns,
        own_part[:, :low_rank_product] * factor,
        own_part[:, low_rank_product:] * factor,
    )


def solution(mesh):
    placed = (
        P("batch", "seq", None),
        P("batch", "seq", None),
        P(),
        P(),
        P("batch", "seq"),
        P("batch", "seq"),
        P("batch", "seq"),
        P("batch"),
    )
    return jax.shard_map(
        local,
        mesh=mesh,
        in_specs=placed,
        out_specs=(P("batch", "seq"), P(("batch", "seq"), None), P(("batch", "seq"), None)),
        check_vma=False,
    )
```

profile of v0, /device:TPU:1, one launch (start us, length us, event | category | flops | bytes accessed | tf_op | source)
XLA Modules:
  0.0 333.0 jit_solution(8268280413247830999)
XLA Ops:
  7.2 0.0 copy-start
  8.0 1.8 fusion.6
  9.8 0.5 slice.12
  10.4 1.3 broadcast_in_dim.7
  11.6 8.6 %all-to-all-start = ((f32[32,1,1]{2,1,0:T(1,128)}), f32[32,1,1]{2,1,0:T(1,128)S(1)}, u32[]{:S(2)}, u32[]{:S(2)}) async-start(f32[32,1,1]{2,1,0:T(1,128)} %broadcast_in_dim.7), calls=%async_computation | async-start | bytes 32768 | tf_op jit(solution)/shard_map/all_to_all | solution.py:14
  20.2 0.0 all-reduce.2.cloned.1.call-start
  20.2 0.0 copy-start.1
  20.3 4.3 %fusion.1 = f32[512,256]{0,1:T(8,128)S(1)} fusion(bf16[4096,256]{1,0:T(8,128)(2,1)} %param.11, bf16[1,512,4096]{2,1,0:T(8,128)(2,1)} %param.9), kind=kOutput, calls=%fused_computation.5 | convolution fusion | flops 1073741824 | bytes 6815744 | tf_op jit(solution)/shard_map/ogz,zw->ogw/dot_general | solution.py:44
  24.6 0.0 copy-done
  24.6 0.0 copy-done.1
  24.6 0.0 copy-start.4
  24.6 0.0 copy-start.5
  24.6 1.3 multiply_reduce_fusion.1
  26.0 1.1 all-to-all-done
  27.1 0.3 reduce.3
  27.4 0.6 fusion.26
  28.0 0.7 multiply_add_fusion
  28.7 0.0 copy-start.3
  28.7 0.0 copy-done.4
  28.7 0.0 copy-done.5
  28.7 0.0 copy-start.2
  28.8 3.6 %convolution_bitcast_fusion.1 = f32[4096,256]{0,1:T(8,128)S(1)} fusion(bf16[1,512,4096]{2,1,0:T(8,128)(2,1)} %param.8, f32[512,256]{0,1:T(8,128)S(1)} %fusion.1, f32[512]{0:T(512)S(1)} %bitcast.35), kind=kOutput, calls=%fused_computation.3 | convolution fusion | flops 1074003968 | bytes 8914944 | tf_op jit(solution)/shard_map/oxe,oxq->eq/dot_general | solution.py:79
  32.4 0.0 copy-done.3
  32.4 0.0 copy-done.2
  32.4 1.3 convolution_bitcast_fusion
  33.7 3.8 %pad_maximum_fusion = f32[4096,512]{0,1:T(8,128)} fusion(f32[4096,256]{0,1:T(8,128)S(1)} %convolution_bitcast_fusion, f32[4096,256]{0,1:T(8,128)S(1)} %convolution_bitcast_fusion.1), kind=kLoop, calls=%fused_computation | loop fusion | flops 2097152 | bytes 16777216 | tf_op jit(solution)/shard_map/concatenate | solution.py:77
  37.4 0.0 all-reduce.2.cloned.1.call-update
  37.4 279.3 %all-reduce.2.cloned.1.call-done = f32[4096,512]{0,1:T(8,128)} async-done(((f32[4096,512]{0,1:T(8,128)}), f32[4096,512]{0,1:T(8,128)}) %all-reduce.2.cloned.1.call-update) | async-done | bytes 8388624 | tf_op jit(solution)/shard_map/psum | solution.py:86
  316.8 6.1 %multiply_reduce_fusion = f32[]{:T(128)} fusion(f32[4096,512]{0,1:T(8,128)} %all-reduce.2.cloned.1.call-done), kind=kLoop, calls=%fused_computation.1 | loop fusion | flops 4194303 | bytes 8388612 | tf_op jit(solution)/shard_map/reduce_sum | solution.py:87
  323.7 1.1 dynamic-slice_multiply_fusion
  324.8 0.7 copy.16
  325.5 0.7 copy.15
  (2 shorter events, 0.0 us)
Async XLA Ops:
  7.2 17.4 %copy-start = (bf16[4096,256]{1,0:T(8,128)(2,1)S(1)}, bf16[4096,256]{1,0:T(8,128)(2,1)}, u32[]{:S(2)}) copy-start(bf16[4096,256]{1,0:T(8,128)(2,1)} %param.10) | copy-start | bytes 6291460
  11.6 15.5 %all-to-all-start = ((f32[32,1,1]{2,1,0:T(1,128)}), f32[32,1,1]{2,1,0:T(1,128)S(1)}, u32[]{:S(2)}, u32[]{:S(2)}) async-start(f32[32,1,1]{2,1,0:T(1,128)} %broadcast_in_dim.7), calls=%async_computation | async-start | bytes 32768 | tf_op jit(solution)/shard_map/all_to_all | solution.py:14
  20.2 296.6 %all-reduce.2.cloned.1.call-start = ((), (), s32[]{:S(2)}) async-start(), calls=%async_computation.1 | async-start | bytes 16777216 | tf_op jit(solution)/shard_map/psum | solution.py:86
  20.2 4.3 %copy-start.1 = (bf16[1,512,4096]{2,1,0:T(8,128)(2,1)S(1)}, bf16[1,512,4096]{2,1,0:T(8,128)(2,1)}, u32[]{:S(2)}) copy-start(bf16[1,512,4096]{2,1,0:T(8,128)(2,1)} %param.8) | copy-start | bytes 12582916
  24.6 4.1 %copy-start.4 = (f32[1,512]{1,0:T(1,128)S(1)}, f32[1,512]{1,0:T(1,128)}, u32[]{:S(2)}) copy-start(f32[1,512]{1,0:T(1,128)} %param.13) | copy-start | bytes 6148
  24.6 4.1 %copy-start.5 = (f32[1,512]{1,0:T(1,128)S(1)}, f32[1,512]{1,0:T(1,128)}, u32[]{:S(2)}) copy-start(f32[1,512]{1,0:T(1,128)} %param.14) | copy-start | bytes 6148
  28.7 3.7 %copy-start.3 = (f32[512]{0:T(512)}, f32[512]{0:T(512)S(1)}, u32[]{:S(2)}) copy-start(f32[512]{0:T(512)S(1)} %multiply_add_fusion) | copy-start | bytes 6148
  28.7 3.6 %copy-start.2 = (bf16[1,512,4096]{2,1,0:T(8,128)(2,1)S(1)}, bf16[1,512,4096]{2,1,0:T(8,128)(2,1)}, u32[]{:S(2)}) copy-start(bf16[1,512,4096]{2,1,0:T(8,128)(2,1)} %param.9) | copy-start | bytes 12582916
Sparse Core Ops, SparseCore 0:
  37.5 279.1 all-reduce.1
where the time goes:
time: 334 us; the launch traced here: 333 us
  waiting for transfers between devices  280 us (84%)
  between operations  15.8 us (5%)
  other arithmetic  12.6 us (4%)
  matrix products  12.3 us (4%)
  starting transfers between devices  8.62 us (3%)
    psum x1, waiting for transfers between devices, local(): summed = lax.psum(partial_terms, ('batch', 'seq'))  279 us
    all_to_all x1, starting transfers between devices, sent_to_all(): lax.all_to_all(jnp.broadcast_to(shard[None], (devices, *shard.shape)), ax...  8.58 us
  transfers between devices with their start and end apart: 2, of which 2 were waited for; matrix products, arithmetic and copies ran while one was open for 2% of the time, Pallas kernels for 0%

commit v1 on v0

v1 whole, which is shorter than its diff:
```python
import functools
import math

import jax
import jax.numpy as jnp
from jax import lax
from jax.experimental import pallas as pl
from jax.experimental.pallas import tpu as pltpu
from jax.sharding import PartitionSpec as P

ratio_cap = 2.0
weight_gain = 0.08

SIDE = 4
DEEP = 8
PLANE = 2 * SIDE * SIDE
TOKENS = 512
SLAB = 512
RANK = 256
CHUNKS = 2 * DEEP
LAG_JOIN, LAG_PASS, LAG_TURN, LAG_PASS2, LAG_DONE = 1, 2, 3, 4, 5
MESH = pl.DeviceIdType.MESH


def kernel(
    total_len,
    seq_total,
    hidden,
    direction,
    down_map,
    up_map,
    rewards,
    values,
    log_ratio,
    lengths,
    returns_out,
    down_out,
    up_out,
    acts,
    maps,
    proj,
    scaled,
    part,
    from_core,
    first,
    pass1,
    side1,
    second,
    pass2,
    side2,
    third,
    from_z,
    carry,
    norm_plane,
    norm_z,
    act_sem,
    map_sem,
    core_sem,
    pass1_sem,
    side1_sem,
    pass2_sem,
    side2_sem,
    small_sem,
    send_sem,
):
    z = lax.axis_index("batch")
    me = lax.axis_index("seq")
    core = me % 2
    x = (me // 2) % SIDE
    y = me // (2 * SIDE)
    f = core * y + (1 - core) * x
    s = core * x + (1 - core) * y

    def seq_of(f_at, s_at):
        y_at = core * f_at + (1 - core) * s_at
        x_at = core * s_at + (1 - core) * f_at
        return (y_at * SIDE + x_at) * 2 + core

    partner = me + 1 - 2 * core
    f_right, f_left = seq_of((f + 1) % SIDE, s), seq_of((f + SIDE - 1) % SIDE, s)
    s_right, s_left = seq_of(f, (s + 1) % SIDE), seq_of(f, (s + SIDE - 1) % SIDE)

    def load(g, k):
        src, table = (hidden, down_map) if g == 0 else (direction, up_map)
        columns = pl.ds(pl.multiple_of(k * SLAB, SLAB), SLAB)
        return (
            pltpu.make_async_copy(src.at[0, :, columns], acts.at[g, k], act_sem.at[g, k]),
            pltpu.make_async_copy(table.at[columns, :], maps.at[g, k], map_sem.at[g, k]),
        )

    for k in range(DEEP):
        for g in range(2):
            for copy in load(g, k):
                copy.start()

    barrier = pltpu.get_barrier_semaphore()

    @pl.loop(1, PLANE)
    def _(step):
        pl.semaphore_signal(
            barrier, inc=1, device_id=(z, (me + step) % PLANE), device_id_type=MESH
        )

    @pl.loop(1, DEEP)
    def _(step):
        pl.semaphore_signal(barrier, inc=1, device_id=((z + step) % DEEP, me), device_id_type=MESH)

    lane = lax.broadcasted_iota(jnp.int32, (8, TOKENS), 1)
    length = jnp.zeros((8, TOKENS), jnp.int32) + lengths[0]
    valid = (me * TOKENS + lane < length).astype(jnp.float32)
    within = jnp.broadcast_to(rewards[...], (8, TOKENS)) * valid
    span = 1
    while span < TOKENS:
        moved = pltpu.roll(within, TOKENS - span, 1)
        moved = jnp.where(lane < TOKENS - span, moved, 0.0)
        within = within + math.exp(-span / total_len) * moved
        span *= 2
    carry[me] = jnp.broadcast_to(within[0:1, 0:1], (1, 128))

    pl.semaphore_wait(barrier, PLANE - 1 + DEEP - 1)

    def to_plane(slots, sent, sem, step):
        return pltpu.make_async_remote_copy(
            src_ref=slots.at[me],
            dst_ref=slots.at[me],
            send_sem=send_sem.at[sent],
            recv_sem=small_sem.at[sem],
            device_id=(z, (me + step) % PLANE),
            device_id_type=MESH,
        )

    def to_column(slots, sent, sem, step):
        return pltpu.make_async_remote_copy(
            src_ref=slots.at[z],
            dst_ref=slots.at[z],
            send_sem=send_sem.at[sent],
            recv_sem=small_sem.at[sem],
            device_id=((z + step) % DEEP, me),
            device_id_type=MESH,
        )

    def wait_bytes(ref, sem):
        pltpu.make_async_copy(ref, ref, sem).wait()

    @pl.loop(1, PLANE)
    def _(step):
        to_plane(carry, 0, 0, step).start()

    for k in range(DEEP):
        for g in range(2):
            for copy in load(g, k):
                copy.wait()
            term = jnp.dot(acts[g, k], maps[g, k], preferred_element_type=jnp.float32)
            if k == 0:
                proj[g] = term
            else:
                proj[g] += term

    wait_bytes(carry.at[pl.ds(0, PLANE - 1)], small_sem.at[0])
    block = lax.broadcasted_iota(jnp.int32, (PLANE, 1, 128), 0)
    ahead = (block - me - 1).astype(jnp.float32)
    decay = jnp.exp(-ahead * TOKENS / total_len)
    carried = jnp.sum(jnp.where(block > me, decay * carry[...], 0.0), axis=0)
    carried = jnp.concatenate([carried] * (TOKENS // 128), axis=1)
    tail = jnp.exp(-(TOKENS - lane).astype(jnp.float32) / total_len)
    returns = within + tail * carried
    returns_out[...] = returns[0:1]
    gain = weight_gain * math.sqrt(total_len * RANK / seq_total) / length.astype(jnp.float32)
    base = valid * (returns - values[...]) * gain
    gap = jnp.broadcast_to(log_ratio[...], (8, TOKENS))
    scale = 1.0 / math.sqrt(RANK)
    here = lax.broadcasted_iota(jnp.int32, (128, 128), 0)
    diagonal = here == lax.broadcasted_iota(jnp.int32, (128, 128), 1)

    def upright(row):
        return jnp.sum(jnp.where(diagonal, row, 0.0), axis=1, keepdims=True)

    for b in range(TOKENS // 128):
        rows = slice(b * 128, b * 128 + 128)
        down, up = proj[0, rows], proj[1, rows]
        delta = scale * jnp.sum(down * up, axis=1, keepdims=True)
        weight = jnp.minimum(jnp.exp(upright(gap[0:1, rows]) + delta), ratio_cap)
        weight = -scale * (weight * upright(base[0:1, rows]))
        scaled[0, rows] = (weight * up).astype(jnp.bfloat16)
        scaled[1, rows] = (weight * down).astype(jnp.bfloat16)

    def plane_of(chunk):
        j = chunk // 2
        far = (DEEP - j) // 2
        return (z + DEEP + (2 * (j % 2) - 1) * far) % DEEP

    def core_copy(i):
        return pltpu.make_async_remote_copy(
            src_ref=part.at[i, :, :, 1 - core],
            dst_ref=from_core.at[i],
            send_sem=send_sem.at[1],
            recv_sem=core_sem.at[i],
            device_id=(z, partner),
            device_id_type=MESH,
        )

    def ring(blocks, passed, sides, pass_sems, side_sems, pass_send, side_send, at, right, left, half):
        low, high = pl.ds(0, half), pl.ds(half, half)
        after, before, across = (at + 1) % SIDE, (at + 3) % SIDE, (at + 2) % SIDE

        def copy(src, dst, send, recv, target):
            return pltpu.make_async_remote_copy(
                src_ref=src,
                dst_ref=dst,
                send_sem=send,
                recv_sem=recv,
                device_id=(z, target),
                device_id_type=MESH,
            )

        def begin(i):
            copy(blocks.at[i, across, low], passed.at[i, 0], pass_send, pass_sems.at[i], right).start()
            copy(blocks.at[i, across, high], passed.at[i, 1], pass_send, pass_sems.at[i], left).start()
            copy(blocks.at[i, after, high], sides.at[i, 0, high], side_send, side_sems.at[i], right).start()
            copy(blocks.at[i, before, low], sides.at[i, 1, low], side_send, side_sems.at[i], left).start()

        def forward(i):
            wait_bytes(passed.at[i], pass_sems.at[i])
            blocks[i, after, low] += passed[i, 0]
            copy(blocks.at[i, after, low], sides.at[i, 0, low], side_send, side_sems.at[i], right).start()
            blocks[i, before, high] += passed[i, 1]
            copy(blocks.at[i, before, high], sides.at[i, 1, high], side_send, side_sems.at[i], left).start()

        def finish(i):
            wait_bytes(sides.at[i], side_sems.at[i])
            return blocks[i, at] + sides[i, 0] + sides[i, 1]

        return begin, forward, finish

    begin1, forward1, finish1 = ring(
        first, pass1, side1, pass1_sem, side1_sem, send_sem.at[2], send_sem.at[3], f, f_right, f_left, 2
    )
    begin2, forward2, finish2 = ring(
        second, pass2, side2, pass2_sem, side2_sem, send_sem.at[4], send_sem.at[5], s, s_right, s_left, 1
    )

    @pl.loop(0, CHUNKS + LAG_DONE)
    def _(turn):
        @pl.when(turn < CHUNKS)
        def _():
            i = turn
            g = i % 2
            term = lax.dot_general(
                acts[g, plane_of(i)],
                scaled[g],
                (((0,), (0,)), ((), ())),
                preferred_element_type=jnp.float32,
            )
            part[i] = term.reshape(SIDE, SIDE, 2, 2, 8, RANK)
            core_copy(i).start()

        @pl.when((turn >= LAG_JOIN) & (turn < CHUNKS + LAG_JOIN))
        def _():
            i = turn - LAG_JOIN
            core_copy(i).wait_recv()

            @pl.loop(0, SIDE)
            def _(a):
                for b in range(SIDE):
                    y_at = core * a + (1 - core) * b
                    x_at = core * b + (1 - core) * a
                    first[i, a, b] = part[i, y_at, x_at, core] + from_core[i, y_at, x_at]

            begin1(i)

        @pl.when((turn >= LAG_PASS) & (turn < CHUNKS + LAG_PASS))
        def _():
            forward1(turn - LAG_PASS)

        @pl.when((turn >= LAG_TURN) & (turn < CHUNKS + LAG_TURN))
        def _():
            i = turn - LAG_TURN
            second[i] = finish1(i)
            begin2(i)

        @pl.when((turn >= LAG_PASS2) & (turn < CHUNKS + LAG_PASS2))
        def _():
            forward2(turn - LAG_PASS2)

        @pl.when(turn >= LAG_DONE)
        def _():
            i = turn - LAG_DONE

            @pl.when(i < CHUNKS - 2)
            def _():
                third[i] = finish2(i)
                pltpu.make_async_remote_copy(
                    src_ref=third.at[i],
                    dst_ref=from_z.at[z, i % 2],
                    send_sem=send_sem.at[6],
                    recv_sem=small_sem.at[1],
                    device_id=(plane_of(i), me),
                    device_id_type=MESH,
                ).start()

            @pl.when(i >= CHUNKS - 2)
            def _():
                from_z[z, i % 2] = finish2(i)

    wait_bytes(from_z.at[pl.ds(0, DEEP - 1)], small_sem.at[1])
    total = jnp.sum(from_z[...], axis=0)
    squares = total * total
    squares = squares[:, :, :, :128] + squares[:, :, :, 128:]
    squares = jnp.sum(squares.reshape(4, 8, 128), axis=0)
    norm_plane[me] = jnp.sum(squares, axis=0, keepdims=True)

    @pl.loop(1, PLANE)
    def _(step):
        to_plane(norm_plane, 7, 2, step).start()

    wait_bytes(norm_plane.at[pl.ds(0, PLANE - 1)], small_sem.at[2])
    norm_z[z] = jnp.sum(norm_plane[...], axis=0)

    @pl.loop(1, DEEP)
    def _(step):
        to_column(norm_z, 8, 3, step).start()

    wait_bytes(norm_z.at[pl.ds(0, DEEP - 1)], small_sem.at[3])
    grad_norm = jnp.sqrt(jnp.sum(jnp.sum(norm_z[...], axis=0), axis=1, keepdims=True))
    clip_norm = 0.5 * math.sqrt(2.0 * SLAB * DEEP * RANK)
    factor = clip_norm / jnp.maximum(grad_norm, clip_norm)
    down_out[...] = total[0].reshape(16, RANK) * factor
    up_out[...] = total[1].reshape(16, RANK) * factor

    wait_bytes(carry.at[pl.ds(0, PLANE - 1)], send_sem.at[0])
    wait_bytes(from_core, send_sem.at[1])
    wait_bytes(pass1, send_sem.at[2])
    wait_bytes(side1, send_sem.at[3])
    wait_bytes(pass2, send_sem.at[4])
    wait_bytes(side2, send_sem.at[5])
    wait_bytes(from_z.at[pl.ds(0, DEEP - 1)], send_sem.at[6])
    wait_bytes(norm_plane.at[pl.ds(0, PLANE - 1)], send_sem.at[7])
    wait_bytes(norm_z.at[pl.ds(0, DEEP - 1)], send_sem.at[8])


def local(hidden, direction, down_map, up_map, rewards, values, log_ratio, lengths):
    total_len = TOKENS * PLANE
    tile = (2, 8, RANK)
    f32 = jnp.float32
    dma = pltpu.SemaphoreType.DMA
    in_hbm = pl.BlockSpec(memory_space=pl.ANY)
    in_vmem = pl.BlockSpec(memory_space=pltpu.VMEM)
    return pl.pallas_call(
        functools.partial(kernel, total_len, DEEP),
        out_shape=(
            jax.ShapeDtypeStruct((1, TOKENS), f32),
            jax.ShapeDtypeStruct((16, RANK), f32),
            jax.ShapeDtypeStruct((16, RANK), f32),
        ),
        in_specs=[in_hbm] * 4 + [in_vmem] * 3 + [pl.BlockSpec(memory_space=pltpu.SMEM)],
        out_specs=(in_vmem, in_vmem, in_vmem),
        scratch_shapes=[
            pltpu.VMEM((2, DEEP, TOKENS, SLAB), jnp.bfloat16),
            pltpu.VMEM((2, DEEP, SLAB, RANK), jnp.bfloat16),
            pltpu.VMEM((2, TOKENS, RANK), f32),
            pltpu.VMEM((2, TOKENS, RANK), jnp.bfloat16),
            pltpu.VMEM((CHUNKS, SIDE, SIDE, 2, *tile), f32),
            pltpu.VMEM((CHUNKS, SIDE, SIDE, *tile), f32),
            pltpu.VMEM((CHUNKS, SIDE, SIDE, *tile), f32),
            pltpu.VMEM((CHUNKS, 2, SIDE // 2, *tile), f32),
            pltpu.VMEM((CHUNKS, 2, SIDE, *tile), f32),
            pltpu.VMEM((CHUNKS, SIDE, *tile), f32),
            pltpu.VMEM((CHUNKS, 2, 1, 8, RANK), f32),
            pltpu.VMEM((CHUNKS, 2, *tile), f32),
            pltpu.VMEM((CHUNKS, *tile), f32),
            pltpu.VMEM((DEEP, 2, *tile), f32),
            pltpu.VMEM((PLANE, 1, 128), f32),
            pltpu.VMEM((PLANE, 1, 128), f32),
            pltpu.VMEM((DEEP, 1, 128), f32),
            dma((2, DEEP)),
            dma((2, DEEP)),
            dma((CHUNKS,)),
            dma((CHUNKS,)),
            dma((CHUNKS,)),
            dma((CHUNKS,)),
            dma((CHUNKS,)),
            dma((4,)),
            dma((9,)),
        ],
        compiler_params=pltpu.CompilerParams(
            collective_id=0, has_side_effects=True, vmem_limit_bytes=60 * 1024 * 1024
        ),
    )(hidden, direction, down_map, up_map, rewards, values, log_ratio, lengths)


def solution(mesh):
    placed = (
        P("batch", "seq", None),
        P("batch", "seq", None),
        P(),
        P(),
        P("batch", "seq"),
        P("batch", "seq"),
        P("batch", "seq"),
        P("batch"),
    )
    return jax.shard_map(
        local,
        mesh=mesh,
        in_specs=placed,
        out_specs=(P("batch", "seq"), P(("batch", "seq"), None), P(("batch", "seq"), None)),
        check_vma=False,
    )
```

time: 334 us -> 89.7 us (0.27)
  waiting for transfers between devices: 280 us -> 0 us
  Pallas kernels: 0 us -> 84.2 us
  between operations: 15.8 us -> 1.29 us
  other arithmetic: 12.6 us -> 0 us
  matrix products: 12.3 us -> 0 us
  starting transfers between devices: 8.62 us -> 0 us
    psum x1 -> x0, waiting for transfers between devices: 279 us -> none  [local(): summed = lax.psum(partial_terms, ('batch', 'seq'))]
    pallas_call x0 -> x1, Pallas kernels: none -> 84.2 us  [local(): pl.pallas_call(functools.partial(kernel, total_len, DEEP), out_shape=(jax...]
    dot_general x5 -> x0, matrix products: 12.3 us -> none  [the longest x1 4.3 us: local(): jnp.einsum('ogz,zw->ogw', score_direction, adapter_up, preferred_element_...]
    all_to_all x1 -> x0, starting transfers between devices: 8.58 us -> none  [sent_to_all(): lax.all_to_all(jnp.broadcast_to(shard[None], (devices, *shard.shape)), ax...]
    reduce_sum x2 -> x0, other arithmetic: 6.76 us -> none  [the longest x1 6.14 us: local(): squares = jnp.sum(summed * summed)]
    concatenate x1 -> x0, other arithmetic: 3.75 us -> none  [local(): jnp.concatenate([jnp.einsum('oxe,oxq->eq', hidden, up_scaled_map, preferr...]
  transfers between devices with their start and end apart: 2 -> 0, of which waited for: 2 -> 0; matrix products, arithmetic and copies ran while one was open for 2% -> 0% of each run, Pallas kernels for 0% -> 0%
where the time goes in v1:
time: 89.7 us; the launch traced here: 89.3 us
  Pallas kernels  84.2 us (94%)
  local copies, waits for them, and re-layouts  3.89 us (4%)
  between operations  1.29 us (1%)
    pallas_call x1, Pallas kernels, local(): pl.pallas_call(functools.partial(kernel, total_len, DEEP), out_shape=(jax...  84.2 us
    unnamed x3, local copies, waits for them, and re-layouts  3.89 us

profile of v1, /device:TPU:1, one launch (start us, length us, event | category | flops | bytes accessed | tf_op | source)
XLA Modules:
  0.0 89.3 jit_solution(9575565287173904063)
XLA Ops:
  1.3 84.2 %shard_map.103 = (f32[1,512]{1,0:T(1,128)}, f32[16,256]{1,0:T(8,128)}, f32[16,256]{1,0:T(8,128)}) custom-call(bf16[1,512,4096]{2,1,0:T(8,128)(2,1)} %hidden.1, bf16[1,512,4096]{2,1,0:T(8,128)(2,1)} %direction.1, bf16[4096,256]{1,0:T(8,128)(2,1)} %down_map.1, bf16[4096,256]{1,0:T(8,128)(2,1)} %up_map.1, f32[1,512]{1,0:T(1,128)} %rewards.1, f32[1,512]{1,0:T(1,128)} %values.1, ...), custom_call_target="tpu_custom_call" | custom-call | tf_op jit(solution)/shard_map/pallas_call | solution.py:348
  85.5 1.2 %copy.15 = f32[1,512]{1,0:T(1,128)} copy(f32[1,512]{1,0:T(1,128)} %get-tuple-element.6) | data formatting | bytes 4096
  86.7 1.3 %copy.16 = f32[16,256]{1,0:T(8,128)} copy(f32[16,256]{1,0:T(8,128)} %get-tuple-element.7) | data formatting | bytes 32768
  88.0 1.3 %copy.17 = f32[16,256]{1,0:T(8,128)} copy(f32[16,256]{1,0:T(8,128)} %get-tuple-element.8) | data formatting | bytes 32768

commit v2 on v1

v2 whole, which is shorter than its diff:
```python
import functools
import math

import jax
import jax.numpy as jnp
from jax import lax
from jax.experimental import pallas as pl
from jax.experimental.pallas import tpu as pltpu
from jax.sharding import PartitionSpec as P

ratio_cap = 2.0
weight_gain = 0.08

SIDE = 4
DEEP = 8
PLANE = 2 * SIDE * SIDE
TOKENS = 512
SLAB = 512
RANK = 256
HALF = SIDE // 2
STRAIGHT = 2
RINGED = DEEP - STRAIGHT
MESH = pl.DeviceIdType.MESH


def kernel(
    total_len,
    seq_total,
    hidden,
    direction,
    down_map,
    up_map,
    rewards_in,
    values_in,
    log_ratio_in,
    lengths_in,
    returns_out,
    total_out,
    factor_out,
    rewards,
    values,
    log_ratio,
    lengths,
    row_sem,
    acts,
    maps,
    proj,
    scaled,
    part,
    from_core,
    first_a,
    pass1_a,
    side1_a,
    second_a,
    in2_a,
    third_a,
    first_b,
    pass1_b,
    side1_b,
    second_b,
    in2_b,
    third_b,
    first_d,
    in1_d,
    second_d,
    in2_d,
    third_d,
    column,
    column_in,
    column_last,
    second_c,
    from_z,
    from_plane,
    carry,
    norm_plane,
    norm_z,
    act_sem,
    map_sem,
    core_sem,
    ring_sem,
    straight_sem,
    column_sem,
    small_sem,
    send_sem,
):
    z = lax.axis_index("batch")
    me = lax.axis_index("seq")
    core = me % 2
    x = (me // 2) % SIDE
    y = me // (2 * SIDE)
    f = core * y + (1 - core) * x
    s = core * x + (1 - core) * y

    def seq_of(f_at, s_at):
        y_at = core * f_at + (1 - core) * s_at
        x_at = core * s_at + (1 - core) * f_at
        return (y_at * SIDE + x_at) * 2 + core

    partner = me + 1 - 2 * core
    f_right, f_left = seq_of((f + 1) % SIDE, s), seq_of((f + SIDE - 1) % SIDE, s)
    s_right, s_left = seq_of(f, (s + 1) % SIDE), seq_of(f, (s + SIDE - 1) % SIDE)

    def load(g, k):
        src, table = (hidden, down_map) if g == 0 else (direction, up_map)
        columns = pl.ds(pl.multiple_of(k * SLAB, SLAB), SLAB)
        return (
            pltpu.make_async_copy(src.at[0, :, columns], acts.at[g, k], act_sem.at[g, k]),
            pltpu.make_async_copy(table.at[columns, :], maps.at[g, k], map_sem.at[g, k]),
        )

    barrier = pltpu.get_barrier_semaphore()

    @pl.loop(1, PLANE)
    def _(step):
        pl.semaphore_signal(
            barrier, inc=1, device_id=(z, (me + step) % PLANE), device_id_type=MESH
        )

    @pl.loop(1, DEEP)
    def _(step):
        pl.semaphore_signal(barrier, inc=1, device_id=((z + step) % DEEP, me), device_id_type=MESH)

    rows = (
        pltpu.make_async_copy(rewards_in, rewards, row_sem.at[0]),
        pltpu.make_async_copy(lengths_in, lengths, row_sem.at[1]),
        pltpu.make_async_copy(values_in, values, row_sem.at[2]),
        pltpu.make_async_copy(log_ratio_in, log_ratio, row_sem.at[3]),
    )
    for copy in rows:
        copy.start()

    for k in range(DEEP):
        for g in range(2):
            for copy in load(g, k):
                copy.start()

    for copy in rows:
        copy.wait()

    lane = lax.broadcasted_iota(jnp.int32, (8, TOKENS), 1)
    length = jnp.zeros((8, TOKENS), jnp.int32) + lengths[0]
    valid = (me * TOKENS + lane < length).astype(jnp.float32)
    within = jnp.broadcast_to(rewards[...], (8, TOKENS)) * valid
    span = 1
    while span < TOKENS:
        moved = pltpu.roll(within, TOKENS - span, 1)
        moved = jnp.where(lane < TOKENS - span, moved, 0.0)
        within = within + math.exp(-span / total_len) * moved
        span *= 2
    carry[me] = jnp.broadcast_to(within[0:1, 0:1], (1, 128))

    pl.semaphore_wait(barrier, PLANE - 1 + DEEP - 1)

    def to_plane(slots, sent, sem, step):
        return pltpu.make_async_remote_copy(
            src_ref=slots.at[me],
            dst_ref=slots.at[me],
            send_sem=send_sem.at[sent],
            recv_sem=small_sem.at[sem],
            device_id=(z, (me + step) % PLANE),
            device_id_type=MESH,
        )

    def to_column(slots, sent, sem, step):
        return pltpu.make_async_remote_copy(
            src_ref=slots.at[z],
            dst_ref=slots.at[z],
            send_sem=send_sem.at[sent],
            recv_sem=small_sem.at[sem],
            device_id=((z + step) % DEEP, me),
            device_id_type=MESH,
        )

    def wait_bytes(ref, sem):
        pltpu.make_async_copy(ref, ref, sem).wait()

    @pl.loop(1, PLANE)
    def _(step):
        to_plane(carry, 0, 0, step).start()

    for k in range(DEEP):
        for g in range(2):
            for copy in load(g, k):
                copy.wait()
            term = jnp.dot(acts[g, k], maps[g, k], preferred_element_type=jnp.float32)
            if k == 0:
                proj[g] = term
            else:
                proj[g] += term

    wait_bytes(carry.at[pl.ds(0, PLANE - 1)], small_sem.at[0])
    block = lax.broadcasted_iota(jnp.int32, (PLANE, 1, 128), 0)
    ahead = (block - me - 1).astype(jnp.float32)
    decay = jnp.exp(-ahead * TOKENS / total_len)
    carried = jnp.sum(jnp.where(block > me, decay * carry[...], 0.0), axis=0)
    carried = jnp.concatenate([carried] * (TOKENS // 128), axis=1)
    tail = jnp.exp(-(TOKENS - lane).astype(jnp.float32) / total_len)
    returns = within + tail * carried
    returns_out[...] = returns[0:1]
    gain = weight_gain * math.sqrt(total_len * RANK / seq_total) / length.astype(jnp.float32)
    base = valid * (returns - values[...]) * gain
    gap = jnp.broadcast_to(log_ratio[...], (8, TOKENS))
    scale = 1.0 / math.sqrt(RANK)
    here = lax.broadcasted_iota(jnp.int32, (128, 128), 0)
    diagonal = here == lax.broadcasted_iota(jnp.int32, (128, 128), 1)

    def upright(row):
        return jnp.sum(jnp.where(diagonal, row, 0.0), axis=1, keepdims=True)

    for b in range(TOKENS // 128):
        rows = slice(b * 128, b * 128 + 128)
        down, up = proj[0, rows], proj[1, rows]
        delta = scale * jnp.sum(down * up, axis=1, keepdims=True)
        weight = jnp.minimum(jnp.exp(upright(gap[0:1, rows]) + delta), ratio_cap)
        weight = -scale * (weight * upright(base[0:1, rows]))
        scaled[0, rows] = (weight * up).astype(jnp.bfloat16)
        scaled[1, rows] = (weight * down).astype(jnp.bfloat16)

    def plane_of(i):
        far = (DEEP - i) // 2
        return (z + DEEP + (2 * (i % 2) - 1) * far) % DEEP

    def send(src, dst, sent, received, target):
        pltpu.make_async_remote_copy(
            src_ref=src,
            dst_ref=dst,
            send_sem=send_sem.at[sent],
            recv_sem=received,
            device_id=target,
            device_id_type=MESH,
        ).start()

    def gradient(i, g, at):
        term = lax.dot_general(
            acts[g, plane_of(i)],
            scaled[g],
            (((0,), (0,)), ((), ())),
            preferred_element_type=jnp.float32,
        )
        part[at] = term.reshape(SIDE, SIDE, 2, 2, 8, RANK)
        send(part.at[at, :, :, 1 - core], from_core.at[at], 1, core_sem.at[at], (z, partner))

    def joined(at, a, b):
        y_at = core * a + (1 - core) * b
        x_at = core * b + (1 - core) * a
        return part[at, y_at, x_at, core] + from_core[at, y_at, x_at]

    def ring(blocks, passed, sides, row, at, right, left, low, high):
        after, before, across = (at + 1) % SIDE, (at + 3) % SIDE, (at + 2) % SIDE
        right, left = (z, right), (z, left)
        sent1, sent2 = 9 + 2 * row, 10 + 2 * row

        def begin(i):
            got, kept = ring_sem.at[row, 0, i], ring_sem.at[row, 1, i]
            send(blocks.at[(i, across, *low)], passed.at[i, 0], sent1, got, right)
            send(blocks.at[(i, across, *high)], passed.at[i, 1], sent1, got, left)
            send(blocks.at[(i, after, *high)], sides.at[(i, 0, *high)], sent2, kept, right)
            send(blocks.at[(i, before, *low)], sides.at[(i, 1, *low)], sent2, kept, left)

        def forward(i):
            got, kept = ring_sem.at[row, 0, i], ring_sem.at[row, 1, i]
            wait_bytes(passed.at[i], got)
            blocks[(i, after, *low)] += passed[i, 0]
            send(blocks.at[(i, after, *low)], sides.at[(i, 0, *low)], sent2, kept, right)
            blocks[(i, before, *high)] += passed[i, 1]
            send(blocks.at[(i, before, *high)], sides.at[(i, 1, *high)], sent2, kept, left)

        def finish(i):
            wait_bytes(sides.at[i], ring_sem.at[row, 1, i])
            return blocks[i, at] + sides[i, 0] + sides[i, 1]

        return begin, forward, finish

    def straight(blocks, arrived, row, at, target):
        def begin(i):
            for k in (2, 1, 3):
                other = (at + k) % SIDE
                send(
                    blocks.at[i, other],
                    arrived.at[i, k - 1],
                    13 + row,
                    straight_sem.at[row, i],
                    (z, target(other)),
                )

        def finish(i):
            wait_bytes(arrived.at[i], straight_sem.at[row, i])
            return blocks[i, at] + arrived[i, 0] + arrived[i, 1] + arrived[i, 2]

        return begin, finish

    def on_f(other):
        return seq_of(other, s)

    def on_s(other):
        return seq_of(f, other)

    halves = (pl.ds(0, HALF),), (pl.ds(HALF, HALF),)
    begin1_a, forward1_a, finish1_a = ring(first_a, pass1_a, side1_a, 0, f, f_right, f_left, *halves)
    begin1_b, forward1_b, finish1_b = ring(first_b, pass1_b, side1_b, 1, f, f_right, f_left, *halves)
    begin2_a, finish2_a = straight(second_a, in2_a, 0, s, on_s)
    begin2_b, finish2_b = straight(second_b, in2_b, 1, s, on_s)
    begin1_d, finish1_d = straight(first_d, in1_d, 2, f, on_f)
    begin2_d, finish2_d = straight(second_d, in2_d, 3, s, on_s)

    def product_a(i):
        gradient(i, 1, i)

    def join_a(i):
        wait_bytes(from_core.at[i], core_sem.at[i])

        @pl.loop(0, SIDE)
        def _(a):
            for b in range(SIDE):
                block = joined(i, a, b)
                column[b, plane_of(i), a] = block[0]
                first_a[i, a, b, 0] = block[1]

        begin1_a(i)

    def turn_a(i):
        second_a[i] = finish1_a(i)
        begin2_a(i)

    def done_a(i):
        @pl.when(i < DEEP - 1)
        def _():
            third_a[i] = finish2_a(i)
            send(third_a.at[i], from_z.at[z, pl.ds(0, 1)], 6, small_sem.at[1], (plane_of(i), me))

        @pl.when(i == DEEP - 1)
        def _():
            from_z[z, 0:1] = finish2_a(i)

    def product_b(i):
        gradient(i, 0, DEEP + i)

    def join_b(i):
        wait_bytes(from_core.at[DEEP + i], core_sem.at[DEEP + i])

        @pl.loop(0, SIDE)
        def _(a):
            for b in range(SIDE):
                first_b[i, a, b] = joined(DEEP + i, a, b)

        begin1_b(i)

    def turn_b(i):
        second_b[i] = finish1_b(i)
        begin2_b(i)

    def done_b(i):
        third_b[i] = finish2_b(i)
        send(third_b.at[i], from_z.at[z, pl.ds(1, 2)], 6, small_sem.at[1], (plane_of(i), me))

    def join_d(i):
        at = DEEP + RINGED + i
        wait_bytes(from_core.at[at], core_sem.at[at])

        @pl.loop(0, SIDE)
        def _(a):
            for b in range(SIDE):
                first_d[i, a, b] = joined(at, a, b)

        begin1_d(i)

    def turn_d(i):
        second_d[i] = finish1_d(i)
        begin2_d(i)

    def done_d(i):
        @pl.when(i < STRAIGHT - 1)
        def _():
            third_d[i] = finish2_d(i)
            send(third_d.at[i], from_z.at[z, pl.ds(1, 2)], 6, small_sem.at[1], (plane_of(RINGED + i), me))

        @pl.when(i == STRAIGHT - 1)
        def _():
            from_z[z, 1:3] = finish2_d(i)

    low, high = pl.ds(0, HALF), pl.ds(HALF, HALF)
    z_right, z_left = ((z + 1) % DEEP, me), ((z + DEEP - 1) % DEEP, me)

    def s_of(u):
        return (s + SIDE - 1 - u) % SIDE

    def plane(step):
        return (z + DEEP + step) % DEEP

    def begin_c(u):
        own, got = s_of(u), column_sem.at[u, 0]
        send(column.at[own, plane(4), low], column_in.at[u, 0, 0, 0], 4, got, z_right)
        send(column.at[own, plane(4), high], column_in.at[u, 0, 1, 0], 4, got, z_left)
        send(column.at[own, plane(3), high], column_in.at[u, 0, 0, 1], 4, got, z_right)
        send(column.at[own, plane(-3), low], column_in.at[u, 0, 1, 1], 4, got, z_left)

    def step_c(step):
        def run(u):
            own, got = s_of(u), column_sem.at[u, step]
            wait_bytes(column_in.at[u, step - 1], column_sem.at[u, step - 1])
            column[own, plane(4 - step), low] += column_in[u, step - 1, 0, 0]
            column[own, plane(step - 4), high] += column_in[u, step - 1, 1, 0]
            if step < 3:
                send(column.at[own, plane(4 - step), low], column_in.at[u, step, 0, 0], 4, got, z_right)
                send(column.at[own, plane(step - 4), high], column_in.at[u, step, 1, 0], 4, got, z_left)
                column[own, plane(3 - step), high] += column_in[u, step - 1, 0, 1]
                column[own, plane(step - 3), low] += column_in[u, step - 1, 1, 1]
                send(column.at[own, plane(3 - step), high], column_in.at[u, step, 0, 1], 4, got, z_right)
                send(column.at[own, plane(step - 3), low], column_in.at[u, step, 1, 1], 4, got, z_left)
            else:
                send(column.at[own, plane(1), low], column_last.at[u, 0], 5, got, z_right)
                send(column.at[own, plane(-1), high], column_last.at[u, 1], 5, got, z_left)

        return run

    def turn_c(u):
        own = s_of(u)
        wait_bytes(column_last.at[u], column_sem.at[u, 3])
        second_c[u, low] = column[own, z, low] + column_last[u, 0] + column_in[u, 2, 1, 1]
        second_c[u, high] = column[own, z, high] + column_last[u, 1] + column_in[u, 2, 0, 1]
        for k in range(SIDE):
            other = (f + k) % SIDE

            def share():
                send(
                    second_c.at[u, other],
                    from_plane.at[k * SIDE + SIDE - 1 - u],
                    3,
                    small_sem.at[4],
                    (z, seq_of(other, own)),
                )

            if k == 0:
                pl.when(u < SIDE - 1)(share)
            else:
                share()

        @pl.when(u == SIDE - 1)
        def _():
            from_plane[0] = second_c[u, f]

    schedule = (
        (0, 1, DEEP, product_a),
        (8, 1, DEEP, product_b),
        (2, 1, DEEP, join_a),
        (10, 1, SIDE, begin_c),
        (10, 1, RINGED, join_b),
        (16, 1, STRAIGHT, join_d),
        (15, 1, SIDE, step_c(1)),
        (20, 1, SIDE, step_c(2)),
        (25, 1, SIDE, step_c(3)),
        (30, 1, SIDE, turn_c),
        (8, 1, DEEP, forward1_a),
        (18, 1, RINGED, forward1_b),
        (14, 1, DEEP, turn_a),
        (26, 1, RINGED, turn_b),
        (21, 1, DEEP, done_a),
        (34, 1, RINGED, done_b),
        (30, 1, STRAIGHT, turn_d),
        (40, 1, STRAIGHT, done_d),
    )

    @pl.loop(0, max(start + every * (count - 1) for start, every, count, _ in schedule) + 1)
    def _(turn):
        for start, every, count, stage in schedule:
            now = (turn >= start) & (turn < start + every * count)
            if every > 1:
                now = now & ((turn - start) % every == 0)
            pl.when(now)(functools.partial(stage, (turn - start) // every))

    wait_bytes(from_z.at[pl.ds(0, DEEP - 1)], small_sem.at[1])
    wait_bytes(from_plane.at[pl.ds(1, SIDE * SIDE - 1)], small_sem.at[4])
    summed = jnp.sum(from_z[...], axis=0)
    total = jnp.concatenate([summed[1:3], jnp.sum(from_plane[...], axis=0)[None], summed[0:1]], axis=0)
    squares = total * total
    squares = jnp.sum(squares[:, :, :128] + squares[:, :, 128:], axis=0)
    norm_plane[me] = jnp.sum(squares, axis=0, keepdims=True)

    @pl.loop(1, PLANE)
    def _(step):
        to_plane(norm_plane, 7, 2, step).start()

    wait_bytes(norm_plane.at[pl.ds(0, PLANE - 1)], small_sem.at[2])
    norm_z[z] = jnp.sum(norm_plane[...], axis=0)

    @pl.loop(1, DEEP)
    def _(step):
        to_column(norm_z, 8, 3, step).start()

    wait_bytes(norm_z.at[pl.ds(0, DEEP - 1)], small_sem.at[3])
    grad_norm = jnp.sqrt(jnp.sum(jnp.sum(norm_z[...], axis=0), axis=1, keepdims=True))
    clip_norm = 0.5 * math.sqrt(2.0 * SLAB * DEEP * RANK)
    factor = clip_norm / jnp.maximum(grad_norm, clip_norm)
    total_out[...] = total.reshape(2, 16, RANK)
    factor_out[...] = jnp.broadcast_to(factor, (1, 128))

    sends = (
        (0, carry.at[pl.ds(0, PLANE - 1)]),
        (1, from_core),
        (3, from_plane.at[pl.ds(1, SIDE * SIDE - 1)]),
        (4, column_in),
        (5, column_last),
        (6, from_z.at[pl.ds(0, DEEP - 1)]),
        (7, norm_plane.at[pl.ds(0, PLANE - 1)]),
        (8, norm_z.at[pl.ds(0, DEEP - 1)]),
        (9, pass1_a),
        (10, side1_a),
        (11, pass1_b),
        (12, side1_b),
        (13, in2_a),
        (14, in2_b),
        (15, in1_d),
        (16, in2_d),
    )
    for sent, ref in sends:
        wait_bytes(ref, send_sem.at[sent])


def clip(returns, total, factor, returns_out, down_out, up_out):
    returns_out[...] = returns[...]
    down_out[...] = total[0] * factor[0:1, 0:1]
    up_out[...] = total[1] * factor[0:1, 0:1]


def local(hidden, direction, down_map, up_map, rewards, values, log_ratio, lengths):
    total_len = TOKENS * PLANE
    tile = (8, RANK)
    f32 = jnp.float32
    dma = pltpu.SemaphoreType.DMA

    def ring_buffers(chunks, tiles):
        block = (tiles, *tile)
        return (
            pltpu.VMEM((chunks, SIDE, SIDE, *block), f32),
            pltpu.VMEM((chunks, 2, HALF, *block), f32),
            pltpu.VMEM((chunks, 2, SIDE, *block), f32),
            pltpu.VMEM((chunks, SIDE, *block), f32),
            pltpu.VMEM((chunks, SIDE - 1, *block), f32),
            pltpu.VMEM((chunks, *block), f32),
        )

    in_hbm = pl.BlockSpec(memory_space=pl.ANY)
    in_vmem = pl.BlockSpec(memory_space=pltpu.VMEM)
    returns, total, factor = pl.pallas_call(
        functools.partial(kernel, total_len, DEEP),
        out_shape=(
            jax.ShapeDtypeStruct((1, TOKENS), f32),
            jax.ShapeDtypeStruct((2, 16, RANK), f32),
            jax.ShapeDtypeStruct((1, 128), f32),
        ),
        in_specs=[in_hbm] * 8,
        out_specs=(in_vmem, in_vmem, in_vmem),
        scratch_shapes=[
            pltpu.VMEM((1, TOKENS), f32),
            pltpu.VMEM((1, TOKENS), f32),
            pltpu.VMEM((1, TOKENS), f32),
            pltpu.SMEM((1,), jnp.int32),
            dma((4,)),
            pltpu.VMEM((2, DEEP, TOKENS, SLAB), jnp.bfloat16),
            pltpu.VMEM((2, DEEP, SLAB, RANK), jnp.bfloat16),
            pltpu.VMEM((2, TOKENS, RANK), f32),
            pltpu.VMEM((2, TOKENS, RANK), jnp.bfloat16),
            pltpu.VMEM((2 * DEEP, SIDE, SIDE, 2, 2, *tile), f32),
            pltpu.VMEM((2 * DEEP, SIDE, SIDE, 2, *tile), f32),
            *ring_buffers(DEEP, 1),
            *ring_buffers(RINGED, 2),
            pltpu.VMEM((STRAIGHT, SIDE, SIDE, 2, *tile), f32),
            pltpu.VMEM((STRAIGHT, SIDE - 1, SIDE, 2, *tile), f32),
            pltpu.VMEM((STRAIGHT, SIDE, 2, *tile), f32),
            pltpu.VMEM((STRAIGHT, SIDE - 1, 2, *tile), f32),
            pltpu.VMEM((STRAIGHT, 2, *tile), f32),
            pltpu.VMEM((SIDE, DEEP, SIDE, *tile), f32),
            pltpu.VMEM((SIDE, 3, 2, 2, HALF, *tile), f32),
            pltpu.VMEM((SIDE, 2, HALF, *tile), f32),
            pltpu.VMEM((SIDE, SIDE, *tile), f32),
            pltpu.VMEM((DEEP, 3, *tile), f32),
            pltpu.VMEM((SIDE * SIDE, *tile), f32),
            pltpu.VMEM((PLANE, 1, 128), f32),
            pltpu.VMEM((PLANE, 1, 128), f32),
            pltpu.VMEM((DEEP, 1, 128), f32),
            dma((2, DEEP)),
            dma((2, DEEP)),
            dma((2 * DEEP,)),
            dma((2, 2, DEEP)),
            dma((4, DEEP)),
            dma((SIDE, 4)),
            dma((5,)),
            dma((17,)),
        ],
        compiler_params=pltpu.CompilerParams(
            collective_id=0, has_side_effects=True, vmem_limit_bytes=60 * 1024 * 1024
        ),
    )(hidden, direction, down_map, up_map, rewards, values, log_ratio, lengths)
    return pl.pallas_call(
        clip,
        out_shape=(
            jax.ShapeDtypeStruct((1, TOKENS), f32),
            jax.ShapeDtypeStruct((16, RANK), f32),
            jax.ShapeDtypeStruct((16, RANK), f32),
        ),
        in_specs=[in_vmem] * 3,
        out_specs=(in_vmem, in_vmem, in_vmem),
    )(returns, total, factor)


def solution(mesh):
    placed = (
        P("batch", "seq", None),
        P("batch", "seq", None),
        P(),
        P(),
        P("batch", "seq"),
        P("batch", "seq"),
        P("batch", "seq"),
        P("batch"),
    )
    return jax.shard_map(
        local,
        mesh=mesh,
        in_specs=placed,
        out_specs=(P("batch", "seq"), P(("batch", "seq"), None), P(("batch", "seq"), None)),
        check_vma=False,
    )
```

time: 89.7 us -> 62.6 us (0.70)
  Pallas kernels: 84.2 us -> 61.1 us
  local copies, waits for them, and re-layouts: 3.89 us -> 0 us
    pallas_call x1, Pallas kernels: 84.2 us -> 59.7 us  [local(): pl.pallas_call(functools.partial(kernel, total_len, DEEP), out_shape=(jax...]
    unnamed x3 -> x0, local copies, waits for them, and re-layouts: 3.89 us -> none
    pallas_call x0 -> x1, Pallas kernels: none -> 1.44 us  [local(): pl.pallas_call(clip, out_shape=(jax.ShapeDtypeStruct((1, TOKENS), f32), j...]
where the time goes in v2:
time: 62.6 us; the launch traced here: 62.4 us
  Pallas kernels  61.1 us (98%)
  between operations  1.29 us (2%)
    pallas_call x1, Pallas kernels, local(): pl.pallas_call(functools.partial(kernel, total_len, DEEP), out_shape=(jax...  59.7 us
    pallas_call x1, Pallas kernels, local(): pl.pallas_call(clip, out_shape=(jax.ShapeDtypeStruct((1, TOKENS), f32), j...  1.44 us

profile of v2, /device:TPU:1, one launch (start us, length us, event | category | flops | bytes accessed | tf_op | source)
XLA Modules:
  0.0 62.4 jit_solution(6488909133943357265)
XLA Ops:
  1.3 59.7 %shard_map.103 = (f32[1,512]{1,0:T(1,128)}, f32[2,16,256]{2,1,0:T(8,128)}, f32[1,128]{1,0:T(1,128)}) custom-call(bf16[1,512,4096]{2,1,0:T(8,128)(2,1)} %hidden.1, bf16[1,512,4096]{2,1,0:T(8,128)(2,1)} %direction.1, bf16[4096,256]{1,0:T(8,128)(2,1)} %down_map.1, bf16[4096,256]{1,0:T(8,128)(2,1)} %up_map.1, f32[1,512]{1,0:T(1,128)} %rewards_in.1, ...), custom_call_target="tpu_custom_call" | custom-call | tf_op jit(solution)/shard_map/pallas_call | solution.py:544
  61.0 1.4 %shard_map.104 = (f32[1,512]{1,0:T(1,128)}, f32[16,256]{1,0:T(8,128)}, f32[16,256]{1,0:T(8,128)}) custom-call(f32[1,512]{1,0:T(1,128)} %get-tuple-element.6.returns, f32[2,16,256]{2,1,0:T(8,128)} %get-tuple-element.7.total, f32[1,128]{1,0:T(1,128)} %get-tuple-element.8.factor), custom_call_target="tpu_custom_call" | custom-call | tf_op jit(solution)/shard_map/pallas_call | solution.py:594

commit v3 on v2

--- a/solution.py
+++ b/solution.py
@@ -446,18 +446,18 @@
         (10, 1, SIDE, begin_c),
         (10, 1, RINGED, join_b),
         (16, 1, STRAIGHT, join_d),
-        (15, 1, SIDE, step_c(1)),
-        (20, 1, SIDE, step_c(2)),
-        (25, 1, SIDE, step_c(3)),
-        (30, 1, SIDE, turn_c),
+        (16, 1, SIDE, step_c(1)),
+        (22, 1, SIDE, step_c(2)),
+        (28, 1, SIDE, step_c(3)),
+        (33, 1, SIDE, turn_c),
         (8, 1, DEEP, forward1_a),
-        (18, 1, RINGED, forward1_b),
+        (17, 1, RINGED, forward1_b),
         (14, 1, DEEP, turn_a),
-        (26, 1, RINGED, turn_b),
+        (25, 1, RINGED, turn_b),
         (21, 1, DEEP, done_a),
-        (34, 1, RINGED, done_b),
-        (30, 1, STRAIGHT, turn_d),
-        (40, 1, STRAIGHT, done_d),
+        (33, 1, RINGED, done_b),
+        (31, 1, STRAIGHT, turn_d),
+        (41, 1, STRAIGHT, done_d),
     )
 
     @pl.loop(0, max(start + every * (count - 1) for start, every, count, _ in schedule) + 1)

time: 62.6 us -> 62 us (level)
  no operation moved by 1% of the time
where the time goes in v3:
time: 62 us; the launch traced here: 61.8 us
  Pallas kernels  60.5 us (98%)
  between operations  1.29 us (2%)
    pallas_call x1, Pallas kernels, local(): pl.pallas_call(functools.partial(kernel, total_len, DEEP), out_shape=(jax...  59.1 us
    pallas_call x1, Pallas kernels, local(): pl.pallas_call(clip, out_shape=(jax.ShapeDtypeStruct((1, TOKENS), f32), j...  1.44 us

profile of v3, /device:TPU:1, one launch (start us, length us, event | category | flops | bytes accessed | tf_op | source)
XLA Modules:
  0.0 61.8 jit_solution(2269265782826469401)
XLA Ops:
  1.3 59.1 %shard_map.103 = (f32[1,512]{1,0:T(1,128)}, f32[2,16,256]{2,1,0:T(8,128)}, f32[1,128]{1,0:T(1,128)}) custom-call(bf16[1,512,4096]{2,1,0:T(8,128)(2,1)} %hidden.1, bf16[1,512,4096]{2,1,0:T(8,128)(2,1)} %direction.1, bf16[4096,256]{1,0:T(8,128)(2,1)} %down_map.1, bf16[4096,256]{1,0:T(8,128)(2,1)} %up_map.1, f32[1,512]{1,0:T(1,128)} %rewards_in.1, ...), custom_call_target="tpu_custom_call" | custom-call | tf_op jit(solution)/shard_map/pallas_call | solution.py:544
  60.4 1.4 %shard_map.104 = (f32[1,512]{1,0:T(1,128)}, f32[16,256]{1,0:T(8,128)}, f32[16,256]{1,0:T(8,128)}) custom-call(f32[1,512]{1,0:T(1,128)} %get-tuple-element.6.returns, f32[2,16,256]{2,1,0:T(8,128)} %get-tuple-element.7.total, f32[1,128]{1,0:T(1,128)} %get-tuple-element.8.factor), custom_call_target="tpu_custom_call" | custom-call | tf_op jit(solution)/shard_map/pallas_call | solution.py:594
